TPU v7x, 32 devices: a whole 2x2x4 slice. The times are simulated.
32 devices in a mesh: seq: 16 (over z, y, x), tp: 2 (over core).
Axes of the slice: x: 2, y: 2, z: 4, core: 2. Of those that a mesh axis runs over, the one named last changes fastest.
Arguments:
- img_qkv: bfloat16 [1, 512, 3, 2048], P(None, 'seq', None, 'tp'), may hold values from -7 to 7
- txt_qkv: bfloat16 [1, 256, 3, 2048], P(None, None, None, 'tp'), may hold values from -7 to 7
- frame_index: int32 [1, 512], P(None, 'seq'), may hold values from 0 to 32
- row_index: int32 [1, 512], P(None, 'seq'), may hold values from 0 to 44
- column_index: int32 [1, 512], P(None, 'seq'), may hold values from 0 to 79
- txt_len: int32 [1], replicated, may hold values from 64 to 256
- residual: bfloat16 [1, 512, 3072], P(None, ('seq', 'tp')), may hold values from -6 to 6
- w_proj: bfloat16 [2048, 3072], P('tp'), may hold values from -0.125 to 0.125
- proj_bias: float32 [3072], replicated, may hold values from -3 to 3
- gate: float32 [3072], replicated, may hold values from -4 to 4
Outputs:
- img_out: bfloat16 [1, 512, 3072], P(None, ('seq', 'tp'))
- txt_out: bfloat16 [1, 256, 2048], P(None, None, 'tp')
All inputs are finite; a program needn't handle non-finite values.
Results may differ from a plain program's by a relative error of at most 0.0082.
Values may be sent and summed in bfloat16 or wider, within the bound.
A program may use at most 64 MiB of HBM per device.

v0:
```python
import math
import jax
import jax.numpy as jnp
from jax import lax
from jax.sharding import PartitionSpec as P

HD = 128
rope_base = 256.0
neg_large = -1e30


def rope_tables(frame_index, row_index, column_index, head_dim):
    frame_part = head_dim // 8
    second = (head_dim - frame_part) // 2
    pieces = []
    for places, part_width in (
        (frame_index, frame_part),
        (row_index, second),
        (column_index, second),
    ):
        pair_ids = jnp.arange(part_width // 2).astype(jnp.float32)
        pair_rates = rope_base ** (-2.0 * pair_ids / part_width)
        pieces.append(places.astype(jnp.float32)[:, None] * pair_rates[None, :])
    angles = jnp.repeat(jnp.concatenate(pieces, axis=1), 2, axis=1)
    parity = jnp.arange(head_dim) % 2
    signed = jnp.where(parity == 0, -1.0, 1.0).astype(jnp.float32)
    return (jnp.cos(angles), jnp.sin(angles) * signed[None, :])


def rotate(block_in, cosine, sine_table):
    values = block_in.astype(jnp.float32)
    parity = jnp.arange(values.shape[-1]) % 2
    partner = jnp.where(parity == 0, jnp.roll(values, -1, axis=-1), jnp.roll(values, 1, axis=-1))
    return (values * cosine[:, None, :] + partner * sine_table[:, None, :]).astype(jnp.bfloat16)


def absorb(carry_state, queries, block_keys, block_values, live_keys, score_scale):
    peak, weight_sum, blended = carry_state
    scores = (
        jnp.einsum("cqd,ckd->cqk", queries, block_keys, preferred_element_type=jnp.float32)
        * score_scale
    )
    if live_keys is not None:
        scores = jnp.where(live_keys[:, None, :], scores, neg_large)
    new_peak = jnp.maximum(peak, jnp.max(scores, axis=2))
    weights = jnp.exp(scores - new_peak[:, :, None])
    if live_keys is not None:
        weights = jnp.where(live_keys[:, None, :], weights, 0.0)
    shrink = jnp.exp(peak - new_peak)
    weight_sum = weight_sum * shrink + jnp.sum(weights, axis=2)
    blended = blended * shrink[:, :, None] + jnp.einsum(
        "cqk,ckd->cqd",
        weights.astype(jnp.bfloat16),
        block_values,
        preferred_element_type=jnp.float32,
    )
    return (new_peak, weight_sum, blended)


def shards(
    img_qkv,
    txt_qkv,
    frame_index,
    row_index,
    column_index,
    txt_len,
    residual,
    w_proj,
    proj_bias,
    gate,
):
    clips = img_qkv.shape[0]
    clip_tok = img_qkv.shape[1]
    head_dim = HD
    heads_tp = img_qkv.shape[3] // head_dim
    seq_count = lax.axis_size("seq")
    tp_count = lax.axis_size("tp")
    groups = seq_count // heads_tp
    per_group = clip_tok // groups
    txt_total = txt_qkv.shape[1]
    txt_share = txt_total // groups
    position = lax.axis_index("seq")
    my_head = position % heads_tp
    my_group = position // heads_tp
    score_scale = 1.0 / math.sqrt(head_dim)
    cosine, sine_table = rope_tables(
        frame_index.reshape(-1), row_index.reshape(-1), column_index.reshape(-1), head_dim
    )
    img_query = rotate(
        img_qkv[:, :, 0].reshape(clips * clip_tok, heads_tp, head_dim), cosine, sine_table
    ).reshape(clips, clip_tok, heads_tp, head_dim)
    img_key = rotate(
        img_qkv[:, :, 1].reshape(clips * clip_tok, heads_tp, head_dim), cosine, sine_table
    ).reshape(clips, clip_tok, heads_tp, head_dim)
    img_value = img_qkv[:, :, 2].reshape(clips, clip_tok, heads_tp, head_dim)
    query_send = (
        img_query.reshape(clips, groups, per_group, heads_tp, head_dim)
        .transpose(1, 3, 0, 2, 4)
        .reshape(seq_count, clips * per_group, head_dim)
    )
    key_value = jnp.stack([img_key, img_value], axis=2)
    txt_head = lax.dynamic_slice_in_dim(txt_qkv, my_head * head_dim, head_dim, 3)
    txt_query = lax.dynamic_slice_in_dim(txt_head[:, :, 0], my_group * txt_share, txt_share, 1)
    img_rows_count = seq_count * per_group
    query_rows = img_rows_count + txt_share
    start_state = (
        jnp.full((clips, query_rows), neg_large, jnp.float32),
        jnp.zeros((clips, query_rows), jnp.float32),
        jnp.zeros((clips, query_rows, head_dim), jnp.float32),
    )
    copies = jnp.broadcast_to(
        key_value.transpose(3, 0, 1, 2, 4)[None], (groups, heads_tp, clips, clip_tok, 2, head_dim)
    ).reshape(seq_count, clips, clip_tok, 2, head_dim)
    query_recv, pair_recv = (
        lax.all_to_all(query_send, "seq", split_axis=0, concat_axis=0, tiled=True),
        lax.all_to_all(copies, "seq", split_axis=0, concat_axis=0, tiled=True),
    )
    ordered = (
        query_recv.reshape(seq_count, clips, per_group, head_dim)
        .transpose(1, 0, 2, 3)
        .reshape(clips, img_rows_count, head_dim)
    )
    queries = jnp.concatenate([ordered, txt_query], axis=1)
    sources = max(1, min(seq_count, 2048 // clip_tok))
    while seq_count % sources:
        sources -= 1
    all_pairs = pair_recv.transpose(1, 0, 2, 3, 4).reshape(
        clips, seq_count // sources, sources * clip_tok, 2, head_dim
    )
    key_blocks = all_pairs.transpose(1, 0, 2, 3, 4)

    def sweep_block(carry_state, key_block):
        return (
            absorb(carry_state, queries, key_block[:, :, 0], key_block[:, :, 1], None, score_scale),
            None,
        )

    carry_state, unused = lax.scan(sweep_block, start_state, key_blocks)
    txt_live = jnp.arange(txt_total)[None, :] < txt_len[:, None]
    peak, weight_sum, blended = absorb(
        carry_state, queries, txt_head[:, :, 1], txt_head[:, :, 2], txt_live, score_scale
    )
    attended = (blended / weight_sum[:, :, None]).astype(jnp.bfloat16)
    img_part = (
        attended[:, :img_rows_count]
        .reshape(clips, seq_count, per_group, head_dim)
        .transpose(1, 0, 2, 3)
    )
    txt_part = attended[:, img_rows_count:]
    returned = lax.all_to_all(img_part, "seq", split_axis=0, concat_axis=0, tiled=True)
    home_rows = (
        returned.reshape(groups, heads_tp, clips, per_group, head_dim)
        .transpose(2, 0, 3, 1, 4)
        .reshape(clips, clip_tok, heads_tp * head_dim)
    )
    txt_index = my_group * txt_share + jnp.arange(txt_share)
    txt_keep = (txt_index[None, :] < txt_len[:, None])[:, :, None]
    txt_part = jnp.where(txt_keep, txt_part, jnp.zeros_like(txt_part))
    gathered = lax.all_gather(txt_part[None], "seq", axis=0, tiled=True)
    txt_out = (
        gathered.reshape(groups, heads_tp, clips, txt_share, head_dim)
        .transpose(2, 0, 3, 1, 4)
        .reshape(clips, txt_total, heads_tp * head_dim)
    )
    row_share = clip_tok // tp_count
    share_rows = clips * row_share
    ordered_rows = (
        home_rows.reshape(clips, tp_count, row_share, heads_tp * head_dim)
        .transpose(1, 0, 2, 3)
        .reshape(tp_count * share_rows, heads_tp * head_dim)
    )
    projected = lax.psum_scatter(
        jnp.dot(ordered_rows, w_proj, preferred_element_type=jnp.float32).astype(jnp.bfloat16),
        "tp",
        scatter_dimension=0,
        tiled=True,
    ).astype(jnp.float32)
    projected = projected.reshape(clips, row_share, projected.shape[1])
    img_out = (
        residual.astype(jnp.float32) + gate[None, None, :] * (projected + proj_bias[None, None, :])
    ).astype(jnp.bfloat16)
    return (img_out, txt_out)


def solution(mesh):
    in_specs = (
        P(None, "seq", None, "tp"),
        P(None, None, None, "tp"),
        P(None, "seq"),
        P(None, "seq"),
        P(None, "seq"),
        P(),
        P(None, ("seq", "tp"), None),
        P("tp", None),
        P(),
        P(),
    )
    out_specs = (P(None, ("seq", "tp"), None), P(None, None, "tp"))
    return jax.shard_map(shards, mesh=mesh, in_specs=in_specs, out_specs=out_specs, check_vma=False)
```

profile of v0, /device:TPU:0, one launch (start us, length us, event | category | flops | bytes accessed | tf_op | source)
XLA Modules:
  0.0 106.6 jit_solution(7230840717838111667)
XLA Ops:
  7.3 1.0 convert_bitcast_fusion.1
  8.9 0.1 sin.17
  9.1 0.2 broadcast_multiply_fusion
  9.6 0.2 fusion.24
  9.7 0.6 copy.53
  10.4 8.3 %all-to-all-start = ((bf16[16,16,128]{2,1,0:T(8,128)(2,1)}), bf16[16,16,128]{2,1,0:T(8,128)(2,1)S(1)}, u32[]{:S(2)}, u32[]{:S(2)}) async-start(bf16[16,16,128]{2,1,0:T(8,128)(2,1)} %bitcast.8), calls=%async_computation | async-start | bytes 131072 | tf_op jit(solution)/shard_map/all_to_all | solution.py:115
  19.5 0.2 copy.56
  20.0 6.2 %all-to-all-done = bf16[16,16,128]{2,1,0:T(8,128)(2,1)S(1)} async-done(((bf16[16,16,128]{2,1,0:T(8,128)(2,1)}), bf16[16,16,128]{2,1,0:T(8,128)(2,1)S(1)}, u32[]{:S(2)}, u32[]{:S(2)}) %all-to-all-start) | async-done | bytes 65568 | tf_op jit(solution)/shard_map/all_to_all | solution.py:115
  26.3 0.8 broadcast_in_dim.105
  27.0 3.5 %all-to-all-start.1 = ((bf16[16,1,32,2,128]{4,2,3,1,0:T(8,128)(2,1)}), bf16[16,1,32,2,128]{4,2,3,1,0:T(8,128)(2,1)S(1)}, u32[]{:S(2)}, u32[]{:S(2)}) async-start(bf16[16,1,32,2,128]{4,2,3,1,0:T(8,128)(2,1)} %bitcast.21), calls=%async_computation.1 | async-start | bytes 524288 | tf_op jit(solution)/shard_map/all_to_all | solution.py:116
  31.3 0.2 fusion.38
  31.5 7.5 %all-to-all-done.1 = bf16[16,1,32,2,128]{4,2,3,1,0:T(8,128)(2,1)S(1)} async-done(((bf16[16,1,32,2,128]{4,2,3,1,0:T(8,128)(2,1)}), bf16[16,1,32,2,128]{4,2,3,1,0:T(8,128)(2,1)S(1)}, u32[]{:S(2)}, u32[]{:S(2)}) %all-to-all-start.1) | async-done | bytes 262176 | tf_op jit(solution)/shard_map/all_to_all | solution.py:116
  39.1 0.3 fusion.37
  39.5 0.3 fusion.5
  39.8 0.3 fusion.2
  40.2 0.3 fusion.4
  40.5 0.6 slice.88
  41.2 3.7 %all-to-all-start.2 = ((bf16[16,1,16,128]{3,2,1,0:T(8,128)(2,1)}), bf16[16,1,16,128]{3,2,1,0:T(8,128)(2,1)S(1)}, u32[]{:S(2)}, u32[]{:S(2)}) async-start(bf16[16,1,16,128]{3,2,1,0:T(8,128)(2,1)} %bitcast.30), calls=%async_computation.2 | async-start | bytes 131072 | tf_op jit(solution)/shard_map/all_to_all | solution.py:150
  44.9 7.5 %all-to-all-done.2 = bf16[16,1,16,128]{3,2,1,0:T(8,128)(2,1)S(1)} async-done(((bf16[16,1,16,128]{3,2,1,0:T(8,128)(2,1)}), bf16[16,1,16,128]{3,2,1,0:T(8,128)(2,1)S(1)}, u32[]{:S(2)}, u32[]{:S(2)}) %all-to-all-start.2) | async-done | bytes 65568 | tf_op jit(solution)/shard_map/all_to_all | solution.py:150
  52.4 4.7 %convolution_convert_fusion = bf16[32,3072]{1,0:T(8,128)(2,1)} fusion(bf16[1024,3072]{1,0:T(8,128)(2,1)} %param.17, bf16[4,8,8,128]{3,2,1,0:T(8,128)(2,1)S(1)} %bitcast.138), kind=kOutput, calls=%fused_computation | convolution fusion | flops 201424896 | bytes 6553600 | tf_op jit(solution)/shard_map/dot_general | solution.py:173
  57.2 39.6 %all-gather = bf16[16,128,128]{2,1,0:T(8,128)(2,1)S(1)} all-gather(bf16[1,128,128]{2,1,0:T(8,128)(2,1)S(1)} %slice_select_fusion), channel_id=2, replica_groups=mesh['seq'=16,'tp'=2] {'seq'}, dimensions={0}, use_global_device_ids=true | all-gather | bytes 557056 | tf_op jit(solution)/shard_map/all_gather | solution.py:159
  96.8 0.3 copy.65
  97.1 1.0 reshape.419
  98.1 1.6 %fusion.12 = bf16[1,16,3072]{2,1,0:T(8,128)(2,1)} fusion(bf16[16,3072]{1,0:T(8,128)(2,1)} %reduce-scatter.2.cloned.1.call-done, bf16[1,16,3072]{2,1,0:T(8,128)(2,1)S(1)} %copy-done.1, f32[3072]{0:T(1024)S(1)} %copy-done.2, f32[3072]{0:T(1024)S(1)} %copy-done.3), kind=kLoop, calls=%fused_computation.18 | loop fusion | flops 294912 | bytes 319488 | tf_op jit(solution)/shard_map/convert_element_type | solution.py:181
  (56 shorter events, 2.3 us)
Async XLA Ops:
  7.2 24.1 %copy-start = (bf16[1,256,3,1024]{3,1,2,0:T(8,128)(2,1)S(1)}, bf16[1,256,3,1024]{3,1,2,0:T(8,128)(2,1)}, u32[]{:S(2)}) copy-start(bf16[1,256,3,1024]{3,1,2,0:T(8,128)(2,1)} %param.11) | copy-start | bytes 4718596
  7.2 1.4 %copy-start.6 = (s32[1,32]{1,0:T(1,128)S(1)}, s32[1,32]{1,0:T(1,128)}, u32[]{:S(2)}) copy-start(s32[1,32]{1,0:T(1,128)} %param.12) | copy-start | bytes 388
  7.2 1.4 %copy-start.4 = (s32[1,32]{1,0:T(1,128)S(1)}, s32[1,32]{1,0:T(1,128)}, u32[]{:S(2)}) copy-start(s32[1,32]{1,0:T(1,128)} %param.14) | copy-start | bytes 388
  7.2 1.4 %copy-start.5 = (s32[1,32]{1,0:T(1,128)S(1)}, s32[1,32]{1,0:T(1,128)}, u32[]{:S(2)}) copy-start(s32[1,32]{1,0:T(1,128)} %param.13) | copy-start | bytes 388
  10.4 15.9 %all-to-all-start = ((bf16[16,16,128]{2,1,0:T(8,128)(2,1)}), bf16[16,16,128]{2,1,0:T(8,128)(2,1)S(1)}, u32[]{:S(2)}, u32[]{:S(2)}) async-start(bf16[16,16,128]{2,1,0:T(8,128)(2,1)} %bitcast.8), calls=%async_computation | async-start | bytes 131072 | tf_op jit(solution)/shard_map/all_to_all | solution.py:115
  27.0 12.0 %all-to-all-start.1 = ((bf16[16,1,32,2,128]{4,2,3,1,0:T(8,128)(2,1)}), bf16[16,1,32,2,128]{4,2,3,1,0:T(8,128)(2,1)S(1)}, u32[]{:S(2)}, u32[]{:S(2)}) async-start(bf16[16,1,32,2,128]{4,2,3,1,0:T(8,128)(2,1)} %bitcast.21), calls=%async_computation.1 | async-start | bytes 524288 | tf_op jit(solution)/shard_map/all_to_all | solution.py:116
  41.2 11.2 %all-to-all-start.2 = ((bf16[16,1,16,128]{3,2,1,0:T(8,128)(2,1)}), bf16[16,1,16,128]{3,2,1,0:T(8,128)(2,1)S(1)}, u32[]{:S(2)}, u32[]{:S(2)}) async-start(bf16[16,1,16,128]{3,2,1,0:T(8,128)(2,1)} %bitcast.30), calls=%async_computation.2 | async-start | bytes 131072 | tf_op jit(solution)/shard_map/all_to_all | solution.py:150
  44.9 53.3 %reduce-scatter.2.cloned.1.call-start = ((), (), s32[]{:S(2)}) async-start(), calls=%async_computation.4 | async-start | bytes 294912 | tf_op jit(solution)/shard_map/reduce_scatter | solution.py:172
  57.1 41.0 %copy-start.1 = (bf16[1,16,3072]{2,1,0:T(8,128)(2,1)S(1)}, bf16[1,16,3072]{2,1,0:T(8,128)(2,1)}, u32[]{:S(2)}) copy-start(bf16[1,16,3072]{2,1,0:T(8,128)(2,1)} %param.16) | copy-start | bytes 294916
  57.1 41.0 %copy-start.2 = (f32[3072]{0:T(1024)S(1)}, f32[3072]{0:T(1024)}, u32[]{:S(2)}) copy-start(f32[3072]{0:T(1024)} %param.18) | copy-start | bytes 36868
  57.1 41.0 %copy-start.3 = (f32[3072]{0:T(1024)S(1)}, f32[3072]{0:T(1024)}, u32[]{:S(2)}) copy-start(f32[3072]{0:T(1024)} %param.19) | copy-start | bytes 36868
Sparse Core Ops, SparseCore 0:
  57.2 4.3 reduce-scatter.1
where the time goes:
time: 107 us
  blocking collectives  39.6 us (37%)
  waiting for transfers between devices  21.2 us (20%)
  starting transfers between devices  15.6 us (15%)
  between operations  15 us (14%)
  matrix products  5.93 us (6%)
  local copies, waits for them, and re-layouts  5.11 us (5%)
  other arithmetic  4.09 us (4%)
    all_gather x1, blocking collectives, shards(): gathered = lax.all_gather(txt_part[None], 'seq', axis=0, tiled=True)  39.6 us
    all_to_all x1, starting transfers between devices, shards(): lax.all_to_all(query_send, 'seq', split_axis=0, concat_axis=0, tiled=True)  8.34 us
    all_to_all x1, waiting for transfers between devices, shards(): lax.all_to_all(copies, 'seq', split_axis=0, concat_axis=0, tiled=True)  7.49 us
    all_to_all x1, waiting for transfers between devices, shards(): lax.all_to_all(img_part, 'seq', split_axis=0, concat_axis=0, tiled=True)  7.47 us
    all_to_all x1, waiting for transfers between devices, shards(): lax.all_to_all(query_send, 'seq', split_axis=0, concat_axis=0, tiled=True)  6.25 us
    dot_general x1, matrix products, shards(): jnp.dot(ordered_rows, w_proj, preferred_element_type=jnp.float32)  4.66 us
    all_to_all x1, starting transfers between devices, shards(): lax.all_to_all(img_part, 'seq', split_axis=0, concat_axis=0, tiled=True)  3.69 us
    all_to_all x1, starting transfers between devices, shards(): lax.all_to_all(copies, 'seq', split_axis=0, concat_axis=0, tiled=True)  3.53 us
  transfers between devices with their start and end apart: 4, of which 3 were waited for; matrix products, arithmetic and copies ran while one was open for 3% of the time, Pallas kernels for 0%

commit v1 on v0

--- a/solution.py
+++ b/solution.py
@@ -156,7 +156,14 @@
     txt_index = my_group * txt_share + jnp.arange(txt_share)
     txt_keep = (txt_index[None, :] < txt_len[:, None])[:, :, None]
     txt_part = jnp.where(txt_keep, txt_part, jnp.zeros_like(txt_part))
-    gathered = lax.all_gather(txt_part[None], "seq", axis=0, tiled=True)
+    own = txt_part[None]
+    peers = lax.axis_size("seq")
+    held, blocks = (own, [own])
+    for _ in range(peers - 1):
+        held = lax.ppermute(held, "seq", [(i, (i + 1) % peers) for i in range(peers)])
+        blocks.insert(0, held)
+    merged = jnp.concatenate(blocks, axis=0)
+    gathered = jnp.roll(merged, (lax.axis_index("seq") + 1) * own.shape[0], axis=0)
     txt_out = (
         gathered.reshape(groups, heads_tp, clips, txt_share, head_dim)
         .transpose(2, 0, 3, 1, 4)

time: 107 us -> 170 us (1.59)
  waiting for transfers between devices: 21.2 us -> 116 us
  blocking collectives: 39.6 us -> 0 us
  starting transfers between devices: 15.6 us -> 22.4 us
    ppermute x0 -> x15, waiting for transfers between devices: none -> 98 us  [shards(): lax.ppermute(held, 'seq', [(i, (i + 1) % peers) for i in range(peers)])]
    all_gather x1 -> x0, blocking collectives: 39.6 us -> none  [shards(): gathered = lax.all_gather(txt_part[None], 'seq', axis=0, tiled=True)]
    all_to_all x1, waiting for transfers between devices: 7.47 us -> 0.01 us  [shards(): lax.all_to_all(img_part, 'seq', split_axis=0, concat_axis=0, tiled=True)]
    reduce_scatter x1, waiting for transfers between devices: 0.01 us -> 4.28 us  [shards(): lax.psum_scatter(jnp.dot(ordered_rows, w_proj, preferred_element_type=jnp...]
    ppermute x0 -> x15, starting transfers between devices: none -> 3.5 us  [shards(): lax.ppermute(held, 'seq', [(i, (i + 1) % peers) for i in range(peers)])]
    all_to_all x1, starting transfers between devices: 3.69 us -> 7 us  [shards(): lax.all_to_all(img_part, 'seq', split_axis=0, concat_axis=0, tiled=True)]
  transfers between devices with their start and end apart: 4 -> 19, of which waited for: 3 -> 17; matrix products, arithmetic and copies ran while one was open for 3% -> 5% of each run, Pallas kernels for 0% -> 0%
where the time goes in v1:
time: 170 us; the launch traced here: 169 us
  waiting for transfers between devices  116 us (68%)
  starting transfers between devices  22.4 us (13%)
  between operations  15.3 us (9%)
  matrix products  5.94 us (3%)
  local copies, waits for them, and re-layouts  5.49 us (3%)
  other arithmetic  4.26 us (3%)
    ppermute x15, waiting for transfers between devices, shards(): lax.ppermute(held, 'seq', [(i, (i + 1) % peers) for i in range(peers)])  98 us
    all_to_all x1, starting transfers between devices, shards(): lax.all_to_all(query_send, 'seq', split_axis=0, concat_axis=0, tiled=True)  8.34 us
    all_to_all x1, waiting for transfers between devices, shards(): lax.all_to_all(copies, 'seq', split_axis=0, concat_axis=0, tiled=True)  8.13 us
    all_to_all x1, starting transfers between devices, shards(): lax.all_to_all(img_part, 'seq', split_axis=0, concat_axis=0, tiled=True)  7 us
    all_to_all x1, waiting for transfers between devices, shards(): lax.all_to_all(query_send, 'seq', split_axis=0, concat_axis=0, tiled=True)  5.6 us
    dot_general x1, matrix products, shards(): jnp.dot(ordered_rows, w_proj, preferred_element_type=jnp.float32)  4.67 us
    reduce_scatter x1, waiting for transfers between devices, shards(): lax.psum_scatter(jnp.dot(ordered_rows, w_proj, preferred_element_type=jnp...  4.28 us
    all_to_all x1, starting transfers between devices, shards(): lax.all_to_all(copies, 'seq', split_axis=0, concat_axis=0, tiled=True)  3.53 us
  transfers between devices with their start and end apart: 19, of which 17 were waited for; matrix products, arithmetic and copies ran while one was open for 5% of the time, Pallas kernels for 0%

profile of v1, /device:TPU:0, one launch (start us, length us, event | category | flops | bytes accessed | tf_op | source)
XLA Modules:
  0.0 169.4 jit_solution(9270939822013858922)
XLA Ops:
  10.4 8.3 %all-to-all-start = ((bf16[16,16,128]{2,1,0:T(8,128)(2,1)}), bf16[16,16,128]{2,1,0:T(8,128)(2,1)S(1)}, u32[]{:S(2)}, u32[]{:S(2)}) async-start(bf16[16,16,128]{2,1,0:T(8,128)(2,1)} %bitcast.8), calls=%async_computation | async-start | bytes 131072 | tf_op jit(solution)/shard_map/all_to_all | solution.py:115
  20.7 5.6 %all-to-all-done = bf16[16,16,128]{2,1,0:T(8,128)(2,1)S(1)} async-done(((bf16[16,16,128]{2,1,0:T(8,128)(2,1)}), bf16[16,16,128]{2,1,0:T(8,128)(2,1)S(1)}, u32[]{:S(2)}, u32[]{:S(2)}) %all-to-all-start) | async-done | bytes 65568 | tf_op jit(solution)/shard_map/all_to_all | solution.py:115
  27.0 3.5 %all-to-all-start.1 = ((bf16[16,1,32,2,128]{4,2,3,1,0:T(8,128)(2,1)}), bf16[16,1,32,2,128]{4,2,3,1,0:T(8,128)(2,1)S(1)}, u32[]{:S(2)}, u32[]{:S(2)}) async-start(bf16[16,1,32,2,128]{4,2,3,1,0:T(8,128)(2,1)} %bitcast.21), calls=%async_computation.1 | async-start | bytes 524288 | tf_op jit(solution)/shard_map/all_to_all | solution.py:116
  30.9 8.1 %all-to-all-done.1 = bf16[16,1,32,2,128]{4,2,3,1,0:T(8,128)(2,1)S(1)} async-done(((bf16[16,1,32,2,128]{4,2,3,1,0:T(8,128)(2,1)}), bf16[16,1,32,2,128]{4,2,3,1,0:T(8,128)(2,1)S(1)}, u32[]{:S(2)}, u32[]{:S(2)}) %all-to-all-start.1) | async-done | bytes 262176 | tf_op jit(solution)/shard_map/all_to_all | solution.py:116
  40.6 1.5 collective-permute-start
  42.1 6.1 %collective-permute-done = bf16[1,1,128,128]{3,2,1,0:T(8,128)(2,1)S(1)} collective-permute-done((bf16[1,1,128,128]{3,2,1,0:T(8,128)(2,1)S(1)}, bf16[1,1,128,128]{3,2,1,0:T(8,128)(2,1)S(1)}, u32[]{:S(2)}, u32[]{:S(2)}) %collective-permute-start) | collective-permute-done | bytes 32800 | tf_op jit(solution)/shard_map/ppermute | solution.py:163
  48.2 7.5 %collective-permute-done.1 = bf16[1,1,128,128]{3,2,1,0:T(8,128)(2,1)S(1)} collective-permute-done((bf16[1,1,128,128]{3,2,1,0:T(8,128)(2,1)S(1)}, bf16[1,1,128,128]{3,2,1,0:T(8,128)(2,1)S(1)}, u32[]{:S(2)}, u32[]{:S(2)}) %collective-permute-start.1) | collective-permute-done | bytes 32800 | tf_op jit(solution)/shard_map/ppermute | solution.py:163
  55.7 7.5 %collective-permute-done.2 = bf16[1,1,128,128]{3,2,1,0:T(8,128)(2,1)S(1)} collective-permute-done((bf16[1,1,128,128]{3,2,1,0:T(8,128)(2,1)S(1)}, bf16[1,1,128,128]{3,2,1,0:T(8,128)(2,1)S(1)}, u32[]{:S(2)}, u32[]{:S(2)}) %collective-permute-start.2) | collective-permute-done | bytes 32800 | tf_op jit(solution)/shard_map/ppermute | solution.py:163
  63.2 7.5 %collective-permute-done.3 = bf16[1,1,128,128]{3,2,1,0:T(8,128)(2,1)S(1)} collective-permute-done((bf16[1,1,128,128]{3,2,1,0:T(8,128)(2,1)S(1)}, bf16[1,1,128,128]{3,2,1,0:T(8,128)(2,1)S(1)}, u32[]{:S(2)}, u32[]{:S(2)}) %collective-permute-start.3) | collective-permute-done | bytes 32800 | tf_op jit(solution)/shard_map/ppermute | solution.py:163
  70.7 7.5 %collective-permute-done.4 = bf16[1,1,128,128]{3,2,1,0:T(8,128)(2,1)S(1)} collective-permute-done((bf16[1,1,128,128]{3,2,1,0:T(8,128)(2,1)S(1)}, bf16[1,1,128,128]{3,2,1,0:T(8,128)(2,1)S(1)}, u32[]{:S(2)}, u32[]{:S(2)}) %collective-permute-start.4) | collective-permute-done | bytes 32800 | tf_op jit(solution)/shard_map/ppermute | solution.py:163
  78.2 7.5 %collective-permute-done.5 = bf16[1,1,128,128]{3,2,1,0:T(8,128)(2,1)S(1)} collective-permute-done((bf16[1,1,128,128]{3,2,1,0:T(8,128)(2,1)S(1)}, bf16[1,1,128,128]{3,2,1,0:T(8,128)(2,1)S(1)}, u32[]{:S(2)}, u32[]{:S(2)}) %collective-permute-start.5) | collective-permute-done | bytes 32800 | tf_op jit(solution)/shard_map/ppermute | solution.py:163
  85.8 7.5 %collective-permute-done.6 = bf16[1,1,128,128]{3,2,1,0:T(8,128)(2,1)S(1)} collective-permute-done((bf16[1,1,128,128]{3,2,1,0:T(8,128)(2,1)S(1)}, bf16[1,1,128,128]{3,2,1,0:T(8,128)(2,1)S(1)}, u32[]{:S(2)}, u32[]{:S(2)}) %collective-permute-start.6) | collective-permute-done | bytes 32800 | tf_op jit(solution)/shard_map/ppermute | solution.py:163
  93.3 7.5 %collective-permute-done.7 = bf16[1,1,128,128]{3,2,1,0:T(8,128)(2,1)S(1)} collective-permute-done((bf16[1,1,128,128]{3,2,1,0:T(8,128)(2,1)S(1)}, bf16[1,1,128,128]{3,2,1,0:T(8,128)(2,1)S(1)}, u32[]{:S(2)}, u32[]{:S(2)}) %collective-permute-start.7) | collective-permute-done | bytes 32800 | tf_op jit(solution)/shard_map/ppermute | solution.py:163
  100.8 7.8 %collective-permute-done.8 = bf16[1,1,128,128]{3,2,1,0:T(8,128)(2,1)S(1)} collective-permute-done((bf16[1,1,128,128]{3,2,1,0:T(8,128)(2,1)S(1)}, bf16[1,1,128,128]{3,2,1,0:T(8,128)(2,1)S(1)}, u32[]{:S(2)}, u32[]{:S(2)}) %collective-permute-start.8) | collective-permute-done | bytes 32800 | tf_op jit(solution)/shard_map/ppermute | solution.py:163
  108.6 7.7 %collective-permute-done.9 = bf16[1,1,128,128]{3,2,1,0:T(8,128)(2,1)S(1)} collective-permute-done((bf16[1,1,128,128]{3,2,1,0:T(8,128)(2,1)S(1)}, bf16[1,1,128,128]{3,2,1,0:T(8,128)(2,1)S(1)}, u32[]{:S(2)}, u32[]{:S(2)}) %collective-permute-start.9) | collective-permute-done | bytes 32800 | tf_op jit(solution)/shard_map/ppermute | solution.py:163
  116.9 7.0 %all-to-all-start.2 = ((bf16[16,1,16,128]{3,2,1,0:T(8,128)(2,1)}), bf16[16,1,16,128]{3,2,1,0:T(8,128)(2,1)S(1)}, u32[]{:S(2)}, u32[]{:S(2)}) async-start(bf16[16,1,16,128]{3,2,1,0:T(8,128)(2,1)} %bitcast.30), calls=%async_computation.2 | async-start | bytes 131072 | tf_op jit(solution)/shard_map/all_to_all | solution.py:150
  124.0 2.0 %collective-permute-start.11 = (bf16[1,1,128,128]{3,2,1,0:T(8,128)(2,1)S(1)}, bf16[1,1,128,128]{3,2,1,0:T(8,128)(2,1)S(1)}, u32[]{:S(2)}, u32[]{:S(2)}) collective-permute-start(bf16[1,1,128,128]{3,2,1,0:T(8,128)(2,1)S(1)} %collective-permute-done.10), channel_id=1, source_target_pairs={{0,2},{2,4},{4,6},{6,8},{8,10},{10,12},{12,14},{14,16},{16,18},{18... | collective-permute-start | bytes 98312 | tf_op jit(solution)/shard_map/ppermute | solution.py:163
  125.9 6.1 %collective-permute-done.11 = bf16[1,1,128,128]{3,2,1,0:T(8,128)(2,1)S(1)} collective-permute-done((bf16[1,1,128,128]{3,2,1,0:T(8,128)(2,1)S(1)}, bf16[1,1,128,128]{3,2,1,0:T(8,128)(2,1)S(1)}, u32[]{:S(2)}, u32[]{:S(2)}) %collective-permute-start.11) | collective-permute-done | bytes 32800 | tf_op jit(solution)/shard_map/ppermute | solution.py:163
  132.1 7.5 %collective-permute-done.12 = bf16[1,1,128,128]{3,2,1,0:T(8,128)(2,1)S(1)} collective-permute-done((bf16[1,1,128,128]{3,2,1,0:T(8,128)(2,1)S(1)}, bf16[1,1,128,128]{3,2,1,0:T(8,128)(2,1)S(1)}, u32[]{:S(2)}, u32[]{:S(2)}) %collective-permute-start.12) | collective-permute-done | bytes 32800 | tf_op jit(solution)/shard_map/ppermute | solution.py:163
  139.6 7.5 %collective-permute-done.13 = bf16[1,1,128,128]{3,2,1,0:T(8,128)(2,1)S(1)} collective-permute-done((bf16[1,1,128,128]{3,2,1,0:T(8,128)(2,1)S(1)}, bf16[1,1,128,128]{3,2,1,0:T(8,128)(2,1)S(1)}, u32[]{:S(2)}, u32[]{:S(2)}) %collective-permute-start.13) | collective-permute-done | bytes 32800 | tf_op jit(solution)/shard_map/ppermute | solution.py:163
  147.1 4.7 %convolution_convert_fusion = bf16[32,3072]{1,0:T(8,128)(2,1)} fusion(bf16[1024,3072]{1,0:T(8,128)(2,1)} %param.17, bf16[4,8,8,128]{3,2,1,0:T(8,128)(2,1)S(1)} %bitcast.144), kind=kOutput, calls=%fused_computation | convolution fusion | flops 201424896 | bytes 6553600 | tf_op jit(solution)/shard_map/dot_general | solution.py:180
  151.8 2.8 %collective-permute-done.14 = bf16[1,1,128,128]{3,2,1,0:T(8,128)(2,1)S(1)} collective-permute-done((bf16[1,1,128,128]{3,2,1,0:T(8,128)(2,1)S(1)}, bf16[1,1,128,128]{3,2,1,0:T(8,128)(2,1)S(1)}, u32[]{:S(2)}, u32[]{:S(2)}) %collective-permute-start.14) | collective-permute-done | bytes 32800 | tf_op jit(solution)/shard_map/ppermute | solution.py:163
  156.7 4.3 %reduce-scatter.2.cloned.1.call-done = bf16[16,3072]{1,0:T(8,128)(2,1)} async-done(((bf16[32,3072]{1,0:T(8,128)(2,1)}), bf16[16,3072]{1,0:T(8,128)(2,1)}) %reduce-scatter.2.cloned.1.call-update) | async-done | bytes 98320 | tf_op jit(solution)/shard_map/reduce_scatter | solution.py:179
  161.0 1.6 fusion.12
  (118 shorter events, 9.5 us)
Async XLA Ops:
  7.2 23.5 %copy-start = (bf16[1,256,3,1024]{3,1,2,0:T(8,128)(2,1)S(1)}, bf16[1,256,3,1024]{3,1,2,0:T(8,128)(2,1)}, u32[]{:S(2)}) copy-start(bf16[1,256,3,1024]{3,1,2,0:T(8,128)(2,1)} %param.11) | copy-start | bytes 4718596
  7.2 1.4 copy-start.5
  10.4 15.9 %all-to-all-start = ((bf16[16,16,128]{2,1,0:T(8,128)(2,1)}), bf16[16,16,128]{2,1,0:T(8,128)(2,1)S(1)}, u32[]{:S(2)}, u32[]{:S(2)}) async-start(bf16[16,16,128]{2,1,0:T(8,128)(2,1)} %bitcast.8), calls=%async_computation | async-start | bytes 131072 | tf_op jit(solution)/shard_map/all_to_all | solution.py:115
  27.0 12.0 %all-to-all-start.1 = ((bf16[16,1,32,2,128]{4,2,3,1,0:T(8,128)(2,1)}), bf16[16,1,32,2,128]{4,2,3,1,0:T(8,128)(2,1)S(1)}, u32[]{:S(2)}, u32[]{:S(2)}) async-start(bf16[16,1,32,2,128]{4,2,3,1,0:T(8,128)(2,1)} %bitcast.21), calls=%async_computation.1 | async-start | bytes 524288 | tf_op jit(solution)/shard_map/all_to_all | solution.py:116
  40.6 7.6 %collective-permute-start = (bf16[1,1,128,128]{3,2,1,0:T(8,128)(2,1)S(1)}, bf16[1,1,128,128]{3,2,1,0:T(8,128)(2,1)S(1)}, u32[]{:S(2)}, u32[]{:S(2)}) collective-permute-start(bf16[1,1,128,128]{3,2,1,0:T(8,128)(2,1)S(1)} %fusion.25), channel_id=1, source_target_pairs={{0,2},{2,4},{4,6},{6,8},{8,10},{10,12},{12,14},{14,16},{16,18},{18... | collective-permute-start | bytes 98312 | tf_op jit(solution)/shard_map/ppermute | solution.py:163
  48.2 7.5 %collective-permute-start.1 = (bf16[1,1,128,128]{3,2,1,0:T(8,128)(2,1)S(1)}, bf16[1,1,128,128]{3,2,1,0:T(8,128)(2,1)S(1)}, u32[]{:S(2)}, u32[]{:S(2)}) collective-permute-start(bf16[1,1,128,128]{3,2,1,0:T(8,128)(2,1)S(1)} %collective-permute-done), channel_id=1, source_target_pairs={{0,2},{2,4},{4,6},{6,8},{8,10},{10,12},{12,14},{14,16},{16,18},{18... | collective-permute-start | bytes 98312 | tf_op jit(solution)/shard_map/ppermute | solution.py:163
  55.7 7.5 %collective-permute-start.2 = (bf16[1,1,128,128]{3,2,1,0:T(8,128)(2,1)S(1)}, bf16[1,1,128,128]{3,2,1,0:T(8,128)(2,1)S(1)}, u32[]{:S(2)}, u32[]{:S(2)}) collective-permute-start(bf16[1,1,128,128]{3,2,1,0:T(8,128)(2,1)S(1)} %collective-permute-done.1), channel_id=1, source_target_pairs={{0,2},{2,4},{4,6},{6,8},{8,10},{10,12},{12,14},{14,16},{16,18},{18... | collective-permute-start | bytes 98312 | tf_op jit(solution)/shard_map/ppermute | solution.py:163
  63.2 7.5 %collective-permute-start.3 = (bf16[1,1,128,128]{3,2,1,0:T(8,128)(2,1)S(1)}, bf16[1,1,128,128]{3,2,1,0:T(8,128)(2,1)S(1)}, u32[]{:S(2)}, u32[]{:S(2)}) collective-permute-start(bf16[1,1,128,128]{3,2,1,0:T(8,128)(2,1)S(1)} %collective-permute-done.2), channel_id=1, source_target_pairs={{0,2},{2,4},{4,6},{6,8},{8,10},{10,12},{12,14},{14,16},{16,18},{18... | collective-permute-start | bytes 98312 | tf_op jit(solution)/shard_map/ppermute | solution.py:163
  70.7 7.5 %collective-permute-start.4 = (bf16[1,1,128,128]{3,2,1,0:T(8,128)(2,1)S(1)}, bf16[1,1,128,128]{3,2,1,0:T(8,128)(2,1)S(1)}, u32[]{:S(2)}, u32[]{:S(2)}) collective-permute-start(bf16[1,1,128,128]{3,2,1,0:T(8,128)(2,1)S(1)} %collective-permute-done.3), channel_id=1, source_target_pairs={{0,2},{2,4},{4,6},{6,8},{8,10},{10,12},{12,14},{14,16},{16,18},{18... | collective-permute-start | bytes 98312 | tf_op jit(solution)/shard_map/ppermute | solution.py:163
  78.2 7.5 %collective-permute-start.5 = (bf16[1,1,128,128]{3,2,1,0:T(8,128)(2,1)S(1)}, bf16[1,1,128,128]{3,2,1,0:T(8,128)(2,1)S(1)}, u32[]{:S(2)}, u32[]{:S(2)}) collective-permute-start(bf16[1,1,128,128]{3,2,1,0:T(8,128)(2,1)S(1)} %collective-permute-done.4), channel_id=1, source_target_pairs={{0,2},{2,4},{4,6},{6,8},{8,10},{10,12},{12,14},{14,16},{16,18},{18... | collective-permute-start | bytes 98312 | tf_op jit(solution)/shard_map/ppermute | solution.py:163
  85.7 7.5 %collective-permute-start.6 = (bf16[1,1,128,128]{3,2,1,0:T(8,128)(2,1)S(1)}, bf16[1,1,128,128]{3,2,1,0:T(8,128)(2,1)S(1)}, u32[]{:S(2)}, u32[]{:S(2)}) collective-permute-start(bf16[1,1,128,128]{3,2,1,0:T(8,128)(2,1)S(1)} %collective-permute-done.5), channel_id=1, source_target_pairs={{0,2},{2,4},{4,6},{6,8},{8,10},{10,12},{12,14},{14,16},{16,18},{18... | collective-permute-start | bytes 98312 | tf_op jit(solution)/shard_map/ppermute | solution.py:163
  93.3 7.5 %collective-permute-start.7 = (bf16[1,1,128,128]{3,2,1,0:T(8,128)(2,1)S(1)}, bf16[1,1,128,128]{3,2,1,0:T(8,128)(2,1)S(1)}, u32[]{:S(2)}, u32[]{:S(2)}) collective-permute-start(bf16[1,1,128,128]{3,2,1,0:T(8,128)(2,1)S(1)} %collective-permute-done.6), channel_id=1, source_target_pairs={{0,2},{2,4},{4,6},{6,8},{8,10},{10,12},{12,14},{14,16},{16,18},{18... | collective-permute-start | bytes 98312 | tf_op jit(solution)/shard_map/ppermute | solution.py:163
  100.8 7.8 %collective-permute-start.8 = (bf16[1,1,128,128]{3,2,1,0:T(8,128)(2,1)S(1)}, bf16[1,1,128,128]{3,2,1,0:T(8,128)(2,1)S(1)}, u32[]{:S(2)}, u32[]{:S(2)}) collective-permute-start(bf16[1,1,128,128]{3,2,1,0:T(8,128)(2,1)S(1)} %collective-permute-done.7), channel_id=1, source_target_pairs={{0,2},{2,4},{4,6},{6,8},{8,10},{10,12},{12,14},{14,16},{16,18},{18... | collective-permute-start | bytes 98312 | tf_op jit(solution)/shard_map/ppermute | solution.py:163
  108.6 7.7 %collective-permute-start.9 = (bf16[1,1,128,128]{3,2,1,0:T(8,128)(2,1)S(1)}, bf16[1,1,128,128]{3,2,1,0:T(8,128)(2,1)S(1)}, u32[]{:S(2)}, u32[]{:S(2)}) collective-permute-start(bf16[1,1,128,128]{3,2,1,0:T(8,128)(2,1)S(1)} %collective-permute-done.8), channel_id=1, source_target_pairs={{0,2},{2,4},{4,6},{6,8},{8,10},{10,12},{12,14},{14,16},{16,18},{18... | collective-permute-start | bytes 98312 | tf_op jit(solution)/shard_map/ppermute | solution.py:163
  116.3 7.7 %collective-permute-start.10 = (bf16[1,1,128,128]{3,2,1,0:T(8,128)(2,1)S(1)}, bf16[1,1,128,128]{3,2,1,0:T(8,128)(2,1)S(1)}, u32[]{:S(2)}, u32[]{:S(2)}) collective-permute-start(bf16[1,1,128,128]{3,2,1,0:T(8,128)(2,1)S(1)} %collective-permute-done.9), channel_id=1, source_target_pairs={{0,2},{2,4},{4,6},{6,8},{8,10},{10,12},{12,14},{14,16},{16,18},{18... | collective-permute-start | bytes 98312 | tf_op jit(solution)/shard_map/ppermute | solution.py:163
  116.9 22.7 %all-to-all-start.2 = ((bf16[16,1,16,128]{3,2,1,0:T(8,128)(2,1)}), bf16[16,1,16,128]{3,2,1,0:T(8,128)(2,1)S(1)}, u32[]{:S(2)}, u32[]{:S(2)}) async-start(bf16[16,1,16,128]{3,2,1,0:T(8,128)(2,1)} %bitcast.30), calls=%async_computation.2 | async-start | bytes 131072 | tf_op jit(solution)/shard_map/all_to_all | solution.py:150
  123.9 37.1 %reduce-scatter.2.cloned.1.call-start = ((), (), s32[]{:S(2)}) async-start(), calls=%async_computation.4 | async-start | bytes 294912 | tf_op jit(solution)/shard_map/reduce_scatter | solution.py:179
  124.0 8.1 %collective-permute-start.11 = (bf16[1,1,128,128]{3,2,1,0:T(8,128)(2,1)S(1)}, bf16[1,1,128,128]{3,2,1,0:T(8,128)(2,1)S(1)}, u32[]{:S(2)}, u32[]{:S(2)}) collective-permute-start(bf16[1,1,128,128]{3,2,1,0:T(8,128)(2,1)S(1)} %collective-permute-done.10), channel_id=1, source_target_pairs={{0,2},{2,4},{4,6},{6,8},{8,10},{10,12},{12,14},{14,16},{16,18},{18... | collective-permute-start | bytes 98312 | tf_op jit(solution)/shard_map/ppermute | solution.py:163
  132.1 7.5 %collective-permute-start.12 = (bf16[1,1,128,128]{3,2,1,0:T(8,128)(2,1)S(1)}, bf16[1,1,128,128]{3,2,1,0:T(8,128)(2,1)S(1)}, u32[]{:S(2)}, u32[]{:S(2)}) collective-permute-start(bf16[1,1,128,128]{3,2,1,0:T(8,128)(2,1)S(1)} %collective-permute-done.11), channel_id=1, source_target_pairs={{0,2},{2,4},{4,6},{6,8},{8,10},{10,12},{12,14},{14,16},{16,18},{18... | collective-permute-start | bytes 98312 | tf_op jit(solution)/shard_map/ppermute | solution.py:163
  139.6 7.5 %collective-permute-start.13 = (bf16[1,1,128,128]{3,2,1,0:T(8,128)(2,1)S(1)}, bf16[1,1,128,128]{3,2,1,0:T(8,128)(2,1)S(1)}, u32[]{:S(2)}, u32[]{:S(2)}) collective-permute-start(bf16[1,1,128,128]{3,2,1,0:T(8,128)(2,1)S(1)} %collective-permute-done.12), channel_id=1, source_target_pairs={{0,2},{2,4},{4,6},{6,8},{8,10},{10,12},{12,14},{14,16},{16,18},{18... | collective-permute-start | bytes 98312 | tf_op jit(solution)/shard_map/ppermute | solution.py:163
  147.1 7.5 %collective-permute-start.14 = (bf16[1,1,128,128]{3,2,1,0:T(8,128)(2,1)S(1)}, bf16[1,1,128,128]{3,2,1,0:T(8,128)(2,1)S(1)}, u32[]{:S(2)}, u32[]{:S(2)}) collective-permute-start(bf16[1,1,128,128]{3,2,1,0:T(8,128)(2,1)S(1)} %collective-permute-done.13), channel_id=1, source_target_pairs={{0,2},{2,4},{4,6},{6,8},{8,10},{10,12},{12,14},{14,16},{16,18},{18... | collective-permute-start | bytes 98312 | tf_op jit(solution)/shard_map/ppermute | solution.py:163
  155.2 5.7 %copy-start.1 = (bf16[1,16,3072]{2,1,0:T(8,128)(2,1)S(1)}, bf16[1,16,3072]{2,1,0:T(8,128)(2,1)}, u32[]{:S(2)}) copy-start(bf16[1,16,3072]{2,1,0:T(8,128)(2,1)} %param.16) | copy-start | bytes 294916
  155.2 5.7 %copy-start.2 = (f32[3072]{0:T(1024)S(1)}, f32[3072]{0:T(1024)}, u32[]{:S(2)}) copy-start(f32[3072]{0:T(1024)} %param.18) | copy-start | bytes 36868
  155.3 5.7 %copy-start.3 = (f32[3072]{0:T(1024)S(1)}, f32[3072]{0:T(1024)}, u32[]{:S(2)}) copy-start(f32[3072]{0:T(1024)} %param.19) | copy-start | bytes 36868
  (2 other events, 2.7 us)
Sparse Core Ops, SparseCore 0:
  151.9 9.0 reduce-scatter.1
